TPU v7x, 32 devices: a whole 2x2x4 slice. The times are simulated.
32 devices in a mesh: row: 8 (over y, x, core), grp: 4 (over z).
Axes of the slice: x: 2, y: 2, z: 4, core: 2. Of those that a mesh axis runs over, the one named last changes fastest.
Arguments:
- positions: float32 [3, 1024], replicated, may hold values from -0.05 to 9.35, as said below
- detuning: float32 [1024], replicated, may hold values from -1 to 1
- populations: float32 [1024], P('row'), may hold values from 0 to 1
- base: float32 [2, 64, 1024], P(None, 'grp', 'row'), may hold values from -6 to 6
- section: float32 [2, 64, 1024], P(None, 'grp', 'row'), may hold values from -6 to 6
- accum: float32 [2, 64, 1024], P(None, 'grp', 'row'), may hold values from -3 to 3
Outputs:
- next_input: float32 [2, 64, 1024], P(None, 'grp', 'row')
- accum_out: float32 [2, 64, 1024], P(None, 'grp', 'row')
Inputs may be any that keep to these rules, and one draw needn't show every extreme that they name: `positions`: emitter n sits near the lattice point 0.3 * (n % 32, (n // 32) % 32, n // 1024), displaced by at most 0.05 in each coordinate.
All inputs are finite; a program needn't handle non-finite values.
Results may differ from a plain program's by a relative error of at most 0.0003.
Values sent between devices are 32-bit elements; how exact they have to be, the bound alone decides.
A program may use at most 64 MiB of HBM per device.

v0:
```python
import math
import jax
import jax.numpy as jnp
from jax import lax
from jax.sharding import PartitionSpec as P

WAVE_NUMBER = 2.0 * math.pi
TIME_STEP = 0.2


def coupling(pos_rows, pos_cols, row_ids, col_ids):
    offsets = pos_rows[:, :, None] - pos_cols[:, None, :]
    dist_sq = jnp.sum(offsets * offsets, axis=0)
    on_diag = row_ids[:, None] == col_ids[None, :]
    safe_sq = jnp.where(on_diag, 1.0, dist_sq)
    phase = WAVE_NUMBER * jnp.sqrt(safe_sq)
    inverse = 1.0 / phase
    inverse_sq = inverse * inverse
    aligned = offsets[2] * offsets[2] / safe_sq
    quad_real = 1.0 - inverse_sq - aligned * (1.0 - 3.0 * inverse_sq)
    quad_imag = inverse - 3.0 * aligned * inverse
    cosine = jnp.cos(phase)
    sine = jnp.sin(phase)
    h_real = -0.75 * inverse * (cosine * quad_real - sine * quad_imag)
    h_imag = -0.75 * inverse * (sine * quad_real + cosine * quad_imag)
    return (jnp.where(on_diag, 0.0, h_real), jnp.where(on_diag, 0.0, h_imag))


def cross_rows(slab_part, tile):
    return lax.dot_general(
        slab_part,
        tile,
        (((1,), (1,)), ((), ())),
        precision=lax.Precision.HIGHEST,
        preferred_element_type=jnp.float32,
    )


def lead_rows(tile, slab_part):
    return lax.dot_general(
        tile,
        slab_part,
        (((0,), (0,)), ((), ())),
        precision=lax.Precision.HIGHEST,
        preferred_element_type=jnp.float32,
    )


def slab_rate(
    z_real,
    z_imag,
    shift,
    local_slab,
    full_slab,
    local_det,
    slab_pos,
    slab_det,
    col_start,
    col_count,
):
    slab_ids = lax.iota(jnp.int32, slab_pos.shape[1])
    w_real, w_imag = coupling(slab_pos, slab_pos, slab_ids, slab_ids)
    eye_mask = slab_ids[:, None] == slab_ids[None, :]
    w_real = w_real + jnp.where(eye_mask, slab_det[:, None], 0.0)
    w_imag = w_imag + jnp.where(eye_mask, -0.5, 0.0)
    w_real = lax.dynamic_slice_in_dim(w_real, col_start, col_count, 1)
    w_imag = lax.dynamic_slice_in_dim(w_imag, col_start, col_count, 1)
    v_real = lead_rows(w_real, full_slab[0]) + lead_rows(w_imag, full_slab[1])
    v_imag = lead_rows(w_real, full_slab[1]) - lead_rows(w_imag, full_slab[0])
    y_real = local_slab[0]
    y_imag = local_slab[1]
    z_real = z_real + local_det * y_real + 0.5 * y_imag
    z_imag = z_imag + local_det * y_imag - 0.5 * y_real
    f_real = z_imag + shift * y_imag - v_imag
    f_imag = -z_real - shift * y_real + v_real
    return jnp.stack([f_real, f_imag])


def accumulate(totals, pieces, pos_rows, row_ids, positions):
    slab_piece, pop_piece = pieces
    piece_len = slab_piece.shape[2]
    block_len = math.gcd(piece_len, 512)
    signed_pops = 2.0 * pop_piece.reshape(piece_len) - 1.0

    def one_block(step_index, sums):
        offset = step_index * block_len
        slab_block = lax.dynamic_slice_in_dim(slab_piece, offset, block_len, 2)
        pop_block = lax.dynamic_slice_in_dim(signed_pops, offset, block_len, 0)
        pos_block = lax.dynamic_slice_in_dim(positions, offset, block_len, 1)
        col_ids = offset + lax.iota(jnp.int32, block_len)
        h_real, h_imag = coupling(pos_rows, pos_block, row_ids, col_ids)
        z_real = sums[0] + cross_rows(slab_block[0], h_real) - cross_rows(slab_block[1], h_imag)
        z_imag = sums[1] + cross_rows(slab_block[0], h_imag) + cross_rows(slab_block[1], h_real)
        shift = sums[2] + jnp.dot(h_real, pop_block, precision=lax.Precision.HIGHEST)
        return (z_real, z_imag, shift)

    return lax.fori_loop(0, piece_len // block_len, one_block, totals)


def local(positions, detuning, populations, base, section, accum):
    col_count = section.shape[1]
    slab_width = col_count * lax.axis_size("grp")
    row_count = section.shape[2]
    slab_pos = positions[:, :slab_width]
    slab_det = detuning[:slab_width]
    row_start = lax.axis_index("row") * row_count
    pos_rows = lax.dynamic_slice_in_dim(positions, row_start, row_count, 1)
    local_det = lax.dynamic_slice_in_dim(detuning, row_start, row_count, 0)
    row_ids = row_start + lax.iota(jnp.int32, row_count)
    full_slab = lax.all_gather(section, "grp", axis=1, tiled=True)
    pop_piece = populations.reshape(1, 1, row_count)
    zeros_cols = jnp.zeros((col_count, row_count), jnp.float32)
    initial = (zeros_cols, zeros_cols, jnp.zeros((row_count,), jnp.float32))
    z_real, z_imag, shift = accumulate(
        initial,
        (
            lax.all_gather(section, "row", axis=2, tiled=True),
            lax.all_gather(pop_piece, "row", axis=2, tiled=True),
        ),
        pos_rows,
        row_ids,
        positions,
    )
    col_start = lax.axis_index("grp") * col_count
    rate = slab_rate(
        z_real,
        z_imag,
        shift,
        section,
        full_slab,
        local_det,
        slab_pos,
        slab_det,
        col_start,
        col_count,
    )
    next_input = base + 0.5 * TIME_STEP * rate
    accum_out = accum + TIME_STEP / 3.0 * rate
    return (next_input, accum_out)


def solution(mesh):
    return jax.shard_map(
        local,
        mesh=mesh,
        in_specs=(
            P(),
            P(),
            P("row"),
            P(None, "grp", "row"),
            P(None, "grp", "row"),
            P(None, "grp", "row"),
        ),
        out_specs=(P(None, "grp", "row"), P(None, "grp", "row")),
        check_vma=False,
    )
```

profile of v0, /device:TPU:0, one launch (start us, length us, event | category | flops | bytes accessed | tf_op | source)
XLA Modules:
  0.0 47.5 jit_solution(1856652842638416693)
XLA Ops:
  0.7 0.7 %copy-done.5 = f32[1024]{0:T(1024)S(1)} copy-done((f32[1024]{0:T(1024)S(1)}, f32[1024]{0:T(1024)}, u32[]{:S(2)}) %copy-start.5) | copy-done | bytes 4120
  1.4 0.6 %copy-done.6 = f32[128]{0:T(128)S(1)} copy-done((f32[128]{0:T(128)S(1)}, f32[128]{0:T(128)}, u32[]{:S(2)}) %copy-start.6) | copy-done | bytes 536
  2.1 10.3 %all-gather.1 = f32[8,1,128]{2,1,0:T(1,128)S(1)} all-gather(f32[1,1,128]{2,1,0:T(1,128)S(1)} %bitcast.145), channel_id=2, replica_groups=mesh['row'=8,'grp'=4] {'row'}, dimensions={0}, use_global_device_ids=true | all-gather | bytes 4608 | tf_op jit(solution)/shard_map/all_gather | solution.py:118
  12.4 13.4 %all_gather.11 = f32[2,64,128]{2,1,0:T(8,128)S(1)} all-gather(f32[2,16,128]{2,1,0:T(8,128)S(1)} %copy-done), channel_id=1, replica_groups=mesh['row'=8,'grp'=4] {'grp'}, dimensions={1}, use_global_device_ids=true | all-gather | bytes 81920 | tf_op jit(solution)/shard_map/all_gather | solution.py:110
  25.8 0.1 broadcast_subtract_fusion.1
  25.9 0.2 fusion.52
  26.0 0.6 %slice-done.1 = f32[64]{0:T(128)S(1)} async-done(((f32[1024]{0:T(1024)}), f32[64]{0:T(128)S(1)}, s32[]{:S(2)}) %slice-start.1) | async-done | bytes 280 | tf_op jit(solution)/shard_map/slice | solution.py:105
  26.7 0.1 select_add_fusion
  26.8 0.2 fusion.49
  27.0 0.2 fusion.50
  27.2 9.4 %all_gather.9 = f32[2,16,1024]{2,1,0:T(8,128)S(1)} all-gather(f32[2,16,128]{2,1,0:T(8,128)S(1)} %copy-done), channel_id=1, replica_groups=mesh['row'=8,'grp'=4] {'row'}, dimensions={2}, use_global_device_ids=true | all-gather | bytes 147456 | tf_op jit(solution)/shard_map/all_gather | solution.py:117
  36.7 9.2 %while.18 = (s32[]{:T(128)}, f32[16,128]{1,0:T(8,128)S(1)}, f32[16,128]{1,0:T(8,128)S(1)}, f32[128]{0:T(128)S(1)}, f32[2,16,1024]{2,1,0:T(8,128)S(1)}, /*index=5...) while((s32[]{:T(128)}, f32[16,128]{1,0:T(8,128)S(1)}, ...), condition=%wide.region_2.3_spmd.clone, body=%wide.region_0.2_spmd.clone.sunk | while | flops 54735752 | bytes 3901691 | solution.py:97
  36.7 0.1 dynamic_slice.69
  36.8 0.2 broadcast_subtract_fusion.3
  36.9 1.6 %fusion.83 = f32[128]{0:T(128)S(1)} fusion(f32[512,1]{0,1:T(1,128)S(1)} %bitcast.143, f32[128,512]{1,0:T(8,128)S(1)} %get-tuple-element.288, f32[3,128,512]{2,1,0:T(8,128)S(1)} %get-tuple-element.289, s32[512]{0:T(512)S(1)} %iota_add_fusion.4, s32[128]{0:T(128)S(1)} %iota_add_fusion.5, f32[128]{0:T(128)S(1)} %get-tuple-element.309, pred[]{:T(512)S(6)} %compare.3), kind=kOutput, calls=%fused_computation.6.clone.1 | convolution fusion | flops 2162944 | bytes 529921 | tf_op jit(solution)/shard_map/while/body/eval_jaxpr/dot_general | solution.py:94
  38.5 1.5 %fusion.82 = (f32[128,512]{1,0:T(8,128)S(1)}, f32[128,512]{1,0:T(8,128)S(1)}) fusion(f32[128,512]{1,0:T(8,128)S(1)} %get-tuple-element.288, f32[3,128,512]{2,1,0:T(8,128)S(1)} %get-tuple-element.289, s32[512]{0:T(512)S(1)} %iota_add_fusion.4, s32[128]{0:T(128)S(1)} %iota_add_fusion.5), kind=kLoop, calls=%fused_computation.20.clone.1 | loop fusion | flops 1703936 | bytes 1051136 | tf_op jit(solution)/shard_map/while/body/eval_jaxpr/jit(_where)/select_n | solution.py:26
  40.0 0.3 convolution_add_fusion.7
  40.2 0.3 convolution_subtract_fusion.3
  40.6 0.3 convolution_add_fusion.8
  40.9 0.3 convolution_add_fusion.9
  41.3 0.1 dynamic_slice.69
  41.4 0.2 broadcast_subtract_fusion.3
  41.5 1.6 %fusion.83 = f32[128]{0:T(128)S(1)} fusion(f32[512,1]{0,1:T(1,128)S(1)} %bitcast.143, f32[128,512]{1,0:T(8,128)S(1)} %get-tuple-element.288, f32[3,128,512]{2,1,0:T(8,128)S(1)} %get-tuple-element.289, s32[512]{0:T(512)S(1)} %iota_add_fusion.4, s32[128]{0:T(128)S(1)} %iota_add_fusion.5, f32[128]{0:T(128)S(1)} %get-tuple-element.309, pred[]{:T(512)S(6)} %compare.3), kind=kOutput, calls=%fused_computation.6.clone.1 | convolution fusion | flops 2162944 | bytes 529921 | tf_op jit(solution)/shard_map/while/body/eval_jaxpr/dot_general | solution.py:94
  43.1 1.5 %fusion.82 = (f32[128,512]{1,0:T(8,128)S(1)}, f32[128,512]{1,0:T(8,128)S(1)}) fusion(f32[128,512]{1,0:T(8,128)S(1)} %get-tuple-element.288, f32[3,128,512]{2,1,0:T(8,128)S(1)} %get-tuple-element.289, s32[512]{0:T(512)S(1)} %iota_add_fusion.4, s32[128]{0:T(128)S(1)} %iota_add_fusion.5), kind=kLoop, calls=%fused_computation.20.clone.1 | loop fusion | flops 1703936 | bytes 1051136 | tf_op jit(solution)/shard_map/while/body/eval_jaxpr/jit(_where)/select_n | solution.py:26
  44.6 0.3 convolution_add_fusion.7
  44.8 0.3 convolution_subtract_fusion.3
  45.2 0.3 convolution_add_fusion.8
  45.5 0.3 convolution_add_fusion.9
  45.9 0.2 fusion.44
  46.1 0.2 fusion.46
  46.3 0.5 %copy-done.3 = f32[2,16,128]{2,1,0:T(8,128)S(1)} copy-done((f32[2,16,128]{2,1,0:T(8,128)S(1)}, f32[2,16,128]{2,1,0:T(8,128)}, u32[]{:S(2)}) %copy-start.3) | copy-done | bytes 16408
  46.9 0.6 %multiply_add_fusion = (f32[2,16,128]{2,1,0:T(8,128)}, f32[2,16,128]{2,1,0:T(8,128)}) fusion(f32[2,16,128]{2,1,0:T(8,128)S(1)} %copy-done.3, f32[1,16,128]{2,1,0:T(8,128)S(1)} %fusion.44, f32[1,16,128]{2,1,0:T(8,128)S(1)} %fusion.46, f32[2,16,128]{2,1,0:T(8,128)S(1)} %copy-done.4), kind=kLoop, calls=%fused_computation.90 | loop fusion | flops 20480 | bytes 81920 | tf_op jit(solution)/shard_map/add | solution.py:138
  (27 shorter events, 0.2 us)
Async XLA Ops:
  0.6 0.8 %copy-start.1 = (f32[3,1024]{1,0:T(4,128)S(1)}, f32[3,1024]{1,0:T(4,128)}, u32[]{:S(2)}) copy-start(f32[3,1024]{1,0:T(4,128)} %param.8) | copy-start | bytes 36868
  0.6 0.7 %copy-start.5 = (f32[1024]{0:T(1024)S(1)}, f32[1024]{0:T(1024)}, u32[]{:S(2)}) copy-start(f32[1024]{0:T(1024)} %param.9) | copy-start | bytes 12292
  1.4 0.7 %copy-start.6 = (f32[128]{0:T(128)S(1)}, f32[128]{0:T(128)}, u32[]{:S(2)}) copy-start(f32[128]{0:T(128)} %param.10) | copy-start | bytes 1540
  1.4 11.0 %copy-start = (f32[2,16,128]{2,1,0:T(8,128)S(1)}, f32[2,16,128]{2,1,0:T(8,128)}, u32[]{:S(2)}) copy-start(f32[2,16,128]{2,1,0:T(8,128)} %param.12) | copy-start | bytes 49156
  12.4 13.4 %slice-start = ((f32[3,1024]{1,0:T(4,128)}), f32[3,64]{1,0:T(4,128)S(1)}, s32[]{:S(2)}) async-start(f32[3,1024]{1,0:T(4,128)} %param.8), calls=%async_computation | async-start | bytes 4096 | tf_op jit(solution)/shard_map/slice | solution.py:104
  26.0 0.7 %slice-start.1 = ((f32[1024]{0:T(1024)}), f32[64]{0:T(128)S(1)}, s32[]{:S(2)}) async-start(f32[1024]{0:T(1024)} %param.9), calls=%async_computation.1 | async-start | bytes 1024 | tf_op jit(solution)/shard_map/slice | solution.py:105
  27.2 9.4 %copy-start.2 = (f32[3,1024]{1,0:T(4,128)S(1)}, f32[3,1024]{1,0:T(4,128)}, u32[]{:S(2)}) copy-start(f32[3,1024]{1,0:T(4,128)} %param.8) | copy-start | bytes 36868
  46.1 0.7 %copy-start.3 = (f32[2,16,128]{2,1,0:T(8,128)S(1)}, f32[2,16,128]{2,1,0:T(8,128)}, u32[]{:S(2)}) copy-start(f32[2,16,128]{2,1,0:T(8,128)} %param.13) | copy-start | bytes 49156
  46.1 0.7 %copy-start.4 = (f32[2,16,128]{2,1,0:T(8,128)S(1)}, f32[2,16,128]{2,1,0:T(8,128)}, u32[]{:S(2)}) copy-start(f32[2,16,128]{2,1,0:T(8,128)} %param.11) | copy-start | bytes 49156
where the time goes:
time: 47.9 us; the launch traced here: 47.5 us
  blocking collectives  33 us (69%)
  matrix products  6.46 us (13%)
  other arithmetic  4.29 us (9%)
  local copies, waits for them, and re-layouts  2.78 us (6%)
  between operations  0.77 us (2%)
    all_gather x1, blocking collectives, local(): full_slab = lax.all_gather(section, 'grp', axis=1, tiled=True)  13.4 us
    all_gather x1, blocking collectives, local(): lax.all_gather(pop_piece, 'row', axis=2, tiled=True)  10.3 us
    all_gather x1, blocking collectives, local(): lax.all_gather(section, 'row', axis=2, tiled=True)  9.43 us
    dot_general x2, matrix products, one_block(): jnp.dot(h_real, pop_block, precision=lax.Precision.HIGHEST)  3.13 us
    select_n x2, other arithmetic, coupling(): return (jnp.where(on_diag, 0.0, h_real), jnp.where(on_diag, 0.0, h_imag))  2.93 us
    dot_general x8, matrix products, cross_rows(): lax.dot_general(slab_part, tile, (((1,), (1,)), ((), ())), precision=lax....  2.46 us
    unnamed x14, local copies, waits for them, and re-layouts  1.88 us

commit v1 on v0

--- a/solution.py
+++ b/solution.py
@@ -111,12 +111,10 @@
     pop_piece = populations.reshape(1, 1, row_count)
     zeros_cols = jnp.zeros((col_count, row_count), jnp.float32)
     initial = (zeros_cols, zeros_cols, jnp.zeros((row_count,), jnp.float32))
+    show_roads = lambda shard_in: jnp.concatenate(lax.all_gather(shard_in, "row"), axis=2)
     z_real, z_imag, shift = accumulate(
         initial,
-        (
-            lax.all_gather(section, "row", axis=2, tiled=True),
-            lax.all_gather(pop_piece, "row", axis=2, tiled=True),
-        ),
+        (show_roads(section), lax.all_gather(pop_piece, "row", axis=2, tiled=True)),
         pos_rows,
         row_ids,
         positions,

time: 47.9 us -> 48.4 us (1.010)
  local copies, waits for them, and re-layouts: 2.78 us -> 3.48 us
    unnamed x14, local copies, waits for them, and re-layouts: 1.88 us -> 2.58 us
where the time goes in v1:
time: 48.4 us; the launch traced here: 48 us
  blocking collectives  32.8 us (68%)
  matrix products  6.46 us (13%)
  other arithmetic  4.29 us (9%)
  local copies, waits for them, and re-layouts  3.48 us (7%)
  between operations  0.77 us (2%)
    all_gather x1, blocking collectives, local(): full_slab = lax.all_gather(section, 'grp', axis=1, tiled=True)  13.4 us
    all_gather x1, blocking collectives, local(): lax.all_gather(pop_piece, 'row', axis=2, tiled=True)  10.3 us
    all_gather x1, blocking collectives, local(): lax.all_gather(shard_in, 'row')  9.2 us
    dot_general x2, matrix products, one_block(): jnp.dot(h_real, pop_block, precision=lax.Precision.HIGHEST)  3.13 us
    select_n x2, other arithmetic, coupling(): return (jnp.where(on_diag, 0.0, h_real), jnp.where(on_diag, 0.0, h_imag))  2.93 us
    unnamed x14, local copies, waits for them, and re-layouts  2.58 us
    dot_general x8, matrix products, cross_rows(): lax.dot_general(slab_part, tile, (((1,), (1,)), ((), ())), precision=lax....  2.46 us

profile of v1, /device:TPU:0, one launch (start us, length us, event | category | flops | bytes accessed | tf_op | source)
XLA Modules:
  0.0 48.0 jit_solution(2809724232625520852)
XLA Ops:
  0.7 0.7 %copy-done.5 = f32[1024]{0:T(1024)S(1)} copy-done((f32[1024]{0:T(1024)S(1)}, f32[1024]{0:T(1024)}, u32[]{:S(2)}) %copy-start.5) | copy-done | bytes 4120
  1.4 0.6 %copy-done.6 = f32[128]{0:T(128)S(1)} copy-done((f32[128]{0:T(128)S(1)}, f32[128]{0:T(128)}, u32[]{:S(2)}) %copy-start.6) | copy-done | bytes 536
  2.1 10.3 %all-gather.2 = f32[8,1,128]{2,1,0:T(1,128)S(1)} all-gather(f32[1,1,128]{2,1,0:T(1,128)S(1)} %bitcast.154), channel_id=3, replica_groups=mesh['row'=8,'grp'=4] {'row'}, dimensions={0}, use_global_device_ids=true | all-gather | bytes 4608 | tf_op jit(solution)/shard_map/all_gather | solution.py:117
  12.4 13.4 %all_gather.15 = f32[2,64,128]{2,1,0:T(8,128)S(1)} all-gather(f32[2,16,128]{2,1,0:T(8,128)S(1)} %copy-done), channel_id=1, replica_groups=mesh['row'=8,'grp'=4] {'grp'}, dimensions={1}, use_global_device_ids=true | all-gather | bytes 81920 | tf_op jit(solution)/shard_map/all_gather | solution.py:110
  25.8 0.1 broadcast_subtract_fusion.1
  25.9 0.2 fusion.52
  26.0 0.6 %slice-done.1 = f32[64]{0:T(128)S(1)} async-done(((f32[1024]{0:T(1024)}), f32[64]{0:T(128)S(1)}, s32[]{:S(2)}) %slice-start.1) | async-done | bytes 280 | tf_op jit(solution)/shard_map/slice | solution.py:105
  26.7 0.1 select_add_fusion
  26.8 0.2 fusion.49
  27.0 0.2 fusion.50
  27.2 9.2 %all-gather = f32[16,16,128]{2,1,0:T(8,128)S(1)} all-gather(f32[2,16,128]{2,1,0:T(8,128)S(1)} %copy-done), channel_id=2, replica_groups=mesh['row'=8,'grp'=4] {'row'}, dimensions={0}, use_global_device_ids=true | all-gather | bytes 147456 | tf_op jit(solution)/shard_map/all_gather | solution.py:114
  36.4 0.7 %copy-done.2 = f32[3,1024]{1,0:T(4,128)S(1)} copy-done((f32[3,1024]{1,0:T(4,128)S(1)}, f32[3,1024]{1,0:T(4,128)}, u32[]{:S(2)}) %copy-start.2) | copy-done | bytes 12312
  37.1 9.2 %while.18 = (s32[]{:T(128)}, f32[16,128]{1,0:T(8,128)S(1)}, f32[16,128]{1,0:T(8,128)S(1)}, f32[128]{0:T(128)S(1)}, f32[2,16,1024]{2,1,0:T(8,128)S(1)}, /*index=5...) while((s32[]{:T(128)}, f32[16,128]{1,0:T(8,128)S(1)}, ...), condition=%wide.region_2.3_spmd.clone, body=%wide.region_0.2_spmd.clone.sunk | while | flops 54735752 | bytes 3901691 | solution.py:97
  37.2 0.2 broadcast_subtract_fusion.3
  37.4 1.6 %fusion.83 = f32[128]{0:T(128)S(1)} fusion(f32[512,1]{0,1:T(1,128)S(1)} %bitcast.152, f32[128,512]{1,0:T(8,128)S(1)} %get-tuple-element.288, f32[3,128,512]{2,1,0:T(8,128)S(1)} %get-tuple-element.289, s32[512]{0:T(512)S(1)} %iota_add_fusion.4, s32[128]{0:T(128)S(1)} %iota_add_fusion.5, f32[128]{0:T(128)S(1)} %get-tuple-element.309, pred[]{:T(512)S(6)} %compare.3), kind=kOutput, calls=%fused_computation.6.clone.1 | convolution fusion | flops 2162944 | bytes 529921 | tf_op jit(solution)/shard_map/while/body/eval_jaxpr/dot_general | solution.py:94
  39.0 1.5 %fusion.82 = (f32[128,512]{1,0:T(8,128)S(1)}, f32[128,512]{1,0:T(8,128)S(1)}) fusion(f32[128,512]{1,0:T(8,128)S(1)} %get-tuple-element.288, f32[3,128,512]{2,1,0:T(8,128)S(1)} %get-tuple-element.289, s32[512]{0:T(512)S(1)} %iota_add_fusion.4, s32[128]{0:T(128)S(1)} %iota_add_fusion.5), kind=kLoop, calls=%fused_computation.20.clone.1 | loop fusion | flops 1703936 | bytes 1051136 | tf_op jit(solution)/shard_map/while/body/eval_jaxpr/jit(_where)/select_n | solution.py:26
  40.4 0.3 convolution_add_fusion.7
  40.7 0.3 convolution_subtract_fusion.3
  41.0 0.3 convolution_add_fusion.8
  41.4 0.3 convolution_add_fusion.9
  41.8 0.1 dynamic_slice.69
  41.9 0.2 broadcast_subtract_fusion.3
  42.0 1.6 %fusion.83 = f32[128]{0:T(128)S(1)} fusion(f32[512,1]{0,1:T(1,128)S(1)} %bitcast.152, f32[128,512]{1,0:T(8,128)S(1)} %get-tuple-element.288, f32[3,128,512]{2,1,0:T(8,128)S(1)} %get-tuple-element.289, s32[512]{0:T(512)S(1)} %iota_add_fusion.4, s32[128]{0:T(128)S(1)} %iota_add_fusion.5, f32[128]{0:T(128)S(1)} %get-tuple-element.309, pred[]{:T(512)S(6)} %compare.3), kind=kOutput, calls=%fused_computation.6.clone.1 | convolution fusion | flops 2162944 | bytes 529921 | tf_op jit(solution)/shard_map/while/body/eval_jaxpr/dot_general | solution.py:94
  43.6 1.5 %fusion.82 = (f32[128,512]{1,0:T(8,128)S(1)}, f32[128,512]{1,0:T(8,128)S(1)}) fusion(f32[128,512]{1,0:T(8,128)S(1)} %get-tuple-element.288, f32[3,128,512]{2,1,0:T(8,128)S(1)} %get-tuple-element.289, s32[512]{0:T(512)S(1)} %iota_add_fusion.4, s32[128]{0:T(128)S(1)} %iota_add_fusion.5), kind=kLoop, calls=%fused_computation.20.clone.1 | loop fusion | flops 1703936 | bytes 1051136 | tf_op jit(solution)/shard_map/while/body/eval_jaxpr/jit(_where)/select_n | solution.py:26
  45.1 0.3 convolution_add_fusion.7
  45.3 0.3 convolution_subtract_fusion.3
  45.7 0.3 convolution_add_fusion.8
  46.0 0.3 convolution_add_fusion.9
  46.3 0.2 fusion.44
  46.6 0.2 fusion.46
  46.8 0.5 %copy-done.3 = f32[2,16,128]{2,1,0:T(8,128)S(1)} copy-done((f32[2,16,128]{2,1,0:T(8,128)S(1)}, f32[2,16,128]{2,1,0:T(8,128)}, u32[]{:S(2)}) %copy-start.3) | copy-done | bytes 16408
  47.3 0.6 %multiply_add_fusion = (f32[2,16,128]{2,1,0:T(8,128)}, f32[2,16,128]{2,1,0:T(8,128)}) fusion(f32[2,16,128]{2,1,0:T(8,128)S(1)} %copy-done.3, f32[1,16,128]{2,1,0:T(8,128)S(1)} %fusion.44, f32[1,16,128]{2,1,0:T(8,128)S(1)} %fusion.46, f32[2,16,128]{2,1,0:T(8,128)S(1)} %copy-done.4), kind=kLoop, calls=%fused_computation.91 | loop fusion | flops 20480 | bytes 81920 | tf_op jit(solution)/shard_map/add | solution.py:136
  (28 shorter events, 0.3 us)
Async XLA Ops:
  0.6 0.8 %copy-start.1 = (f32[3,1024]{1,0:T(4,128)S(1)}, f32[3,1024]{1,0:T(4,128)}, u32[]{:S(2)}) copy-start(f32[3,1024]{1,0:T(4,128)} %param.8) | copy-start | bytes 36868
  0.6 0.7 %copy-start.5 = (f32[1024]{0:T(1024)S(1)}, f32[1024]{0:T(1024)}, u32[]{:S(2)}) copy-start(f32[1024]{0:T(1024)} %param.9) | copy-start | bytes 12292
  1.4 0.7 %copy-start.6 = (f32[128]{0:T(128)S(1)}, f32[128]{0:T(128)}, u32[]{:S(2)}) copy-start(f32[128]{0:T(128)} %param.10) | copy-start | bytes 1540
  1.4 11.0 %copy-start = (f32[2,16,128]{2,1,0:T(8,128)S(1)}, f32[2,16,128]{2,1,0:T(8,128)}, u32[]{:S(2)}) copy-start(f32[2,16,128]{2,1,0:T(8,128)} %param.12) | copy-start | bytes 49156
  12.4 13.4 %slice-start = ((f32[3,1024]{1,0:T(4,128)}), f32[3,64]{1,0:T(4,128)S(1)}, s32[]{:S(2)}) async-start(f32[3,1024]{1,0:T(4,128)} %param.8), calls=%async_computation | async-start | bytes 4096 | tf_op jit(solution)/shard_map/slice | solution.py:104
  26.0 0.7 %slice-start.1 = ((f32[1024]{0:T(1024)}), f32[64]{0:T(128)S(1)}, s32[]{:S(2)}) async-start(f32[1024]{0:T(1024)} %param.9), calls=%async_computation.1 | async-start | bytes 1024 | tf_op jit(solution)/shard_map/slice | solution.py:105
  36.4 0.7 %copy-start.2 = (f32[3,1024]{1,0:T(4,128)S(1)}, f32[3,1024]{1,0:T(4,128)}, u32[]{:S(2)}) copy-start(f32[3,1024]{1,0:T(4,128)} %param.8) | copy-start | bytes 36868
  46.6 0.7 %copy-start.3 = (f32[2,16,128]{2,1,0:T(8,128)S(1)}, f32[2,16,128]{2,1,0:T(8,128)}, u32[]{:S(2)}) copy-start(f32[2,16,128]{2,1,0:T(8,128)} %param.13) | copy-start | bytes 49156
  46.6 0.7 %copy-start.4 = (f32[2,16,128]{2,1,0:T(8,128)S(1)}, f32[2,16,128]{2,1,0:T(8,128)}, u32[]{:S(2)}) copy-start(f32[2,16,128]{2,1,0:T(8,128)} %param.11) | copy-start | bytes 49156
